TPU v7x, 32 devices: a whole 2x2x4 slice. The times are simulated.
32 devices in a mesh: tm: 2 (over x), src: 16 (over z, y, core).
Axes of the slice: x: 2, y: 2, z: 4, core: 2. Of those that a mesh axis runs over, the one named last changes fastest.
Arguments:
- design: float32 [16, 524288], P(None, ('tm', 'src')), may hold values from -2 to 2
- unit_index: int32 [524288], P(('tm', 'src')), may hold values from 0 to 255, as said below
- residual: float32 [524288], P(('tm', 'src')), may hold values from -6 to 6
- weight: float32 [524288], P(('tm', 'src')), may hold values from 0.25 to 4
- obs_count: int32 [32], P(('tm', 'src')), may hold values from 1 to 16384, as said below
- damping: float32 [256], P(('tm', 'src')), may hold values from 1 to 10
Outputs:
- solution: float32 [16, 256], P(None, ('tm', 'src'))
- misfit: float32 [], replicated
Inputs may be any that keep to these rules, and one draw needn't show every extreme that they name: `unit_index`: an observation on a device of tm index g names a unit in [g * 128, (g + 1) * 128). `obs_count`: some device has all 16384 slots live.
All inputs are finite; a program needn't handle non-finite values.
Results may differ from a plain program's by a relative error of at most 0.0003.
Values sent between devices are 32-bit elements; how exact they have to be, the bound alone decides.
No kernel may reach another device: no remote copies, remote signals or barrier semaphores. Data moves between devices by JAX's collectives and lax.ppermute only.
A program may use at most 64 MiB of HBM per device.

v0:
```python
import jax
import jax.numpy as jnp
from jax import lax
from jax.sharding import PartitionSpec as P


def make_reader(stacked):

    def reader(row, column):
        return stacked[row * 16 + column]

    return reader


def block_solve(reader, rhs, damping):
    lower = {}
    for j in range(16):
        running = reader(j, j) + damping
        for k in range(j):
            running = running - lower[j, k] * lower[j, k]
        diag_term = jnp.sqrt(running)
        lower[j, j] = diag_term
        for i in range(j + 1, 16):
            running = reader(i, j)
            for k in range(j):
                running = running - lower[i, k] * lower[j, k]
            lower[i, j] = running / diag_term
    forward = []
    for i in range(16):
        running = rhs[i]
        for k in range(i):
            running = running - lower[i, k] * forward[k]
        forward.append(running / lower[i, i])
    backward = [None] * 16
    for i in range(15, -1, -1):
        running = forward[i]
        for k in range(i + 1, 16):
            running = running - lower[k, i] * backward[k]
        backward[i] = running / lower[i, i]
    return jnp.stack(backward)


def quadratic_terms(reader, rhs, solution_own):
    quadratic = jnp.zeros((), jnp.float32)
    for i in range(16):
        applied = jnp.zeros_like(solution_own[0])
        for j in range(16):
            applied = applied + reader(max(i, j), min(i, j)) * solution_own[j]
        quadratic = quadratic + jnp.sum(solution_own[i] * applied)
    return quadratic - 2.0 * jnp.sum(solution_own * rhs)


def on_device(design, unit_index, residual, weight, obs_count, damping):
    n_source = lax.axis_size("src")
    own_units = damping.shape[0]
    units_group = own_units * n_source
    slots = design.shape[1]
    local_unit = unit_index - lax.axis_index("tm") * units_group
    weights_on = jnp.where(
        jnp.arange(slots, dtype=jnp.int32) < obs_count[0], weight, jnp.zeros_like(weight)
    )
    block_rows = 1024
    turns = slots // block_rows
    pair_count = 256

    def pair_rows(rows):
        return (rows[:, None, :] * rows[None, :, :]).reshape(256, rows.shape[1])

    unit_range = jnp.arange(units_group, dtype=jnp.int32)

    def accumulate(step, partial_value):
        begin = step * block_rows
        rows = lax.dynamic_slice_in_dim(design, begin, block_rows, 1)
        units_of = lax.dynamic_slice_in_dim(local_unit, begin, block_rows, 0)
        resid = lax.dynamic_slice_in_dim(residual, begin, block_rows, 0)
        weights_blk = lax.dynamic_slice_in_dim(weights_on, begin, block_rows, 0)
        stacked = jnp.concatenate(
            [pair_rows(rows) * weights_blk, rows * (weights_blk * resid)], axis=0
        )
        one_hot = (units_of[:, None] == unit_range[None, :]).astype(jnp.float32)
        return partial_value + jnp.dot(
            stacked, one_hot, precision=lax.Precision.HIGHEST, preferred_element_type=jnp.float32
        )

    start = jnp.zeros((pair_count + 16, units_group), jnp.float32)
    partial_value = lax.fori_loop(0, turns, accumulate, start)
    own_part = lax.psum_scatter(partial_value, "src", scatter_dimension=1, tiled=True)
    solution_own = block_solve(make_reader(own_part), own_part[pair_count:], damping)
    unit_terms = quadratic_terms(make_reader(own_part), own_part[pair_count:], solution_own)
    before = jnp.sum(weights_on * residual * residual)
    chi_total, weight_total = lax.psum((before + unit_terms, jnp.sum(weights_on)), ("tm", "src"))
    return (solution_own, chi_total / weight_total)


def solution(mesh):
    placed = (
        P(None, ("tm", "src")),
        P(("tm", "src")),
        P(("tm", "src")),
        P(("tm", "src")),
        P(("tm", "src")),
        P(("tm", "src")),
    )
    return jax.shard_map(
        on_device,
        mesh=mesh,
        in_specs=placed,
        out_specs=(P(None, ("tm", "src")), P()),
        check_vma=False,
    )
```

profile of v0, /device:TPU:0, one launch (start us, length us, event | category | flops | bytes accessed | tf_op | source)
XLA Modules:
  0.0 241.2 jit_solution(16647316104159535777)
XLA Ops:
  7.9 0.8 broadcast_subtract_fusion
  8.7 1.6 fusion.56
  10.3 42.7 %while.14 = (s32[]{:T(128)}, f32[272,128]{1,0:T(8,128)S(1)}, f32[16,16384]{1,0:T(8,128)}, f32[16384]{0:T(1024)S(1)}, f32[16384]{0:T(1024)}, /*index=5*/s32[16384...) while((s32[]{:T(128)}, f32[272,128]{1,0:T(8,128)S(1)}, f32[16,16384]{1,0:T(8,128)}, ...), condition=%wide.region_1.2_spmd.clone, body=%wide.region_0.1_spmd.clone.sunk | while | flops 428839936 | bytes 4837545 | solution.py:86
  10.3 0.7 dynamic-slice_multiply_fusion.3
  11.0 0.8 broadcast_multiply_fusion.4
  12.1 0.8 convolution_add_fusion.2
  13.0 0.7 dynamic-slice_multiply_fusion.3
  13.7 0.8 broadcast_multiply_fusion.4
  14.8 0.8 convolution_add_fusion.2
  15.7 0.7 dynamic-slice_multiply_fusion.3
  16.3 0.8 broadcast_multiply_fusion.4
  17.5 0.8 convolution_add_fusion.2
  18.3 0.7 dynamic-slice_multiply_fusion.3
  19.0 0.8 broadcast_multiply_fusion.4
  20.1 0.8 convolution_add_fusion.2
  21.7 0.8 broadcast_multiply_fusion.4
  22.8 0.8 convolution_add_fusion.2
  23.7 0.7 dynamic-slice_multiply_fusion.3
  24.4 0.8 broadcast_multiply_fusion.4
  25.5 0.8 convolution_add_fusion.2
  26.3 0.7 dynamic-slice_multiply_fusion.3
  27.0 0.8 broadcast_multiply_fusion.4
  28.1 0.8 convolution_add_fusion.2
  29.7 0.8 broadcast_multiply_fusion.4
  30.8 0.8 convolution_add_fusion.2
  32.4 0.8 broadcast_multiply_fusion.4
  33.5 0.8 convolution_add_fusion.2
  35.0 0.8 broadcast_multiply_fusion.4
  36.1 0.8 convolution_add_fusion.2
  37.7 0.8 broadcast_multiply_fusion.4
  38.8 0.8 convolution_add_fusion.2
  40.4 0.8 broadcast_multiply_fusion.4
  41.5 0.8 convolution_add_fusion.2
  43.0 0.8 broadcast_multiply_fusion.4
  44.1 0.8 convolution_add_fusion.2
  45.7 0.8 broadcast_multiply_fusion.4
  46.8 0.8 convolution_add_fusion.2
  48.4 0.8 broadcast_multiply_fusion.4
  49.5 0.8 convolution_add_fusion.2
  51.0 0.8 broadcast_multiply_fusion.4
  52.2 0.8 convolution_add_fusion.2
  54.9 90.6 %all-reduce.4.cloned.1.call-done = f32[272,128]{1,0:T(8,128)} async-done(((f32[272,128]{1,0:T(8,128)}), f32[272,128]{1,0:T(8,128)}) %all-reduce.4.cloned.1.call-update) | async-done | bytes 139280
  145.5 1.0 subtract_divide_fusion.110
  146.4 1.2 subtract_sqrt_fusion.8
  147.7 2.8 %subtract_divide_fusion.29 = (f32[8]{0:T(128)S(1)}, f32[8]{0:T(128)S(1)}, f32[8]{0:T(128)S(1)}, f32[8]{0:T(128)S(1)}, f32[8]{0:T(128)S(1)}, /*index=5*/f32[8]{0:...) fusion(f32[272,128]{1,0:T(8,128)} %all-reduce.4.cloned.1.call-d, ...), kind=kLoop, calls=%fused_computation.264 | loop fusion | flops 10472 | bytes 10624 | tf_op jit(solution)/shard_map/div | solution.py:33
  150.5 1.5 subtract_divide_fusion.15
  152.0 1.9 multiply_reduce_fusion
  154.6 1.4 fusion.9
  156.8 1.5 multiply_reduce_fusion.14
  158.2 1.4 multiply_reduce_fusion.15
  161.0 1.5 multiply_reduce_fusion.13
  163.2 1.5 multiply_reduce_fusion.12
  165.3 1.5 multiply_reduce_fusion.11
  167.5 1.5 multiply_reduce_fusion.10
  169.7 1.5 multiply_reduce_fusion.9
  171.8 1.5 multiply_reduce_fusion.8
  174.0 1.5 multiply_reduce_fusion.7
  176.2 1.5 multiply_reduce_fusion.6
  178.3 1.5 multiply_reduce_fusion.5
  180.5 1.5 multiply_reduce_fusion.4
  182.7 1.5 multiply_reduce_fusion.3
  184.8 1.5 multiply_reduce_fusion.2
  187.0 1.5 multiply_reduce_fusion.1
  190.5 41.3 %all-reduce.1 = (f32[]{:T(128)}, f32[]{:T(128)}) all-reduce(f32[]{:T(128)S(6)} %add.1126, f32[]{:T(128)} %get-tuple-element.154), channel_id=1, replica_groups=mesh['tm'=2,'src'=16] {'tm','src'}, use_global_device_ids=true, to_apply=%region_21.22 | all-reduce | flops 2 | bytes 16 | tf_op jit(solution)/shard_map/psum | solution.py:91
  (70 shorter events, 12.9 us)
Async XLA Ops:
  7.2 138.3 %all-reduce.4.cloned.1.call-start = ((), (), s32[]{:S(2)}) async-start(), calls=%async_computation | async-start | bytes 278528
  10.3 43.4 %copy-start.2 = (u32[32]{0:T(128)S(1)}, u32[32]{0:T(128)}, u32[]{:S(2)}) copy-start(u32[32]{0:T(128)} %constant.48) | copy-start | bytes 388
  10.3 135.2 %copy-start.1 = (f32[8]{0:T(128)S(1)}, f32[8]{0:T(128)}, u32[]{:S(2)}) copy-start(f32[8]{0:T(128)} %param.13) | copy-start | bytes 100
  53.0 0.7 copy-start
Sparse Core Ops, SparseCore 0:
  53.8 91.6 all-reduce.3
where the time goes:
time: 244 us; the launch traced here: 241 us
  waiting for transfers between devices  90.6 us (37%)
  other arithmetic  62.9 us (26%)
  blocking collectives  41.3 us (17%)
  between operations  30.2 us (12%)
  matrix products  13.1 us (5%)
    unnamed x2, waiting for transfers between devices  90.6 us
    psum x1, blocking collectives, on_device(): lax.psum((before + unit_terms, jnp.sum(weights_on)), ('tm', 'src'))  41.3 us
    reduce_sum x16, other arithmetic, quadratic_terms(): quadratic = quadratic + jnp.sum(solution_own[i] * applied)  24 us
    mul x16, other arithmetic, accumulate(): rows * (weights_blk * resid)  13.6 us
    dot_general x16, matrix products, accumulate(): jnp.dot(stacked, one_hot, precision=lax.Precision.HIGHEST, preferred_elem...  13.1 us
    mul x16, other arithmetic, accumulate(): weights_blk * resid  11.1 us
  transfers between devices with their start and end apart: 1, of which 1 were waited for; matrix products, arithmetic and copies ran while one was open for 0% of the time, Pallas kernels for 0%

commit v1 on v0

--- a/solution.py
+++ b/solution.py
@@ -2,6 +2,11 @@
 import jax.numpy as jnp
 from jax import lax
 from jax.sharding import PartitionSpec as P
+
+
+def one_after_other(x, one, other):
+    inner = lax.psum(x, one)
+    return lax.psum(inner, other)
 
 
 def make_reader(stacked):
@@ -88,7 +93,9 @@
     solution_own = block_solve(make_reader(own_part), own_part[pair_count:], damping)
     unit_terms = quadratic_terms(make_reader(own_part), own_part[pair_count:], solution_own)
     before = jnp.sum(weights_on * residual * residual)
-    chi_total, weight_total = lax.psum((before + unit_terms, jnp.sum(weights_on)), ("tm", "src"))
+    chi_total, weight_total = one_after_other(
+        (before + unit_terms, jnp.sum(weights_on)), "tm", "src"
+    )
     return (solution_own, chi_total / weight_total)
 
 

time: 244 us -> 239 us (0.980)
  blocking collectives: 41.3 us -> 36.7 us
    psum x1 -> x2, blocking collectives: 41.3 us -> 36.7 us  [the longest x1 31.2 us: one_after_other(): return lax.psum(inner, other)]
where the time goes in v1:
time: 239 us; the launch traced here: 236 us
  waiting for transfers between devices  90.6 us (38%)
  other arithmetic  62.9 us (26%)
  blocking collectives  36.7 us (15%)
  between operations  30 us (13%)
  matrix products  13.1 us (5%)
    unnamed x2, waiting for transfers between devices  90.6 us
    psum x1, blocking collectives, one_after_other(): return lax.psum(inner, other)  31.2 us
    reduce_sum x16, other arithmetic, quadratic_terms(): quadratic = quadratic + jnp.sum(solution_own[i] * applied)  24 us
    mul x16, other arithmetic, accumulate(): rows * (weights_blk * resid)  13.6 us
    dot_general x16, matrix products, accumulate(): jnp.dot(stacked, one_hot, precision=lax.Precision.HIGHEST, preferred_elem...  13.1 us
    mul x16, other arithmetic, accumulate(): weights_blk * resid  11.1 us
    psum x1, blocking collectives, one_after_other(): inner = lax.psum(x, one)  5.52 us
  transfers between devices with their start and end apart: 1, of which 1 were waited for; matrix products, arithmetic and copies ran while one was open for 0% of the time, Pallas kernels for 0%

profile of v1, /device:TPU:0, one launch (start us, length us, event | category | flops | bytes accessed | tf_op | source)
XLA Modules:
  0.0 236.4 jit_solution(5982645079641946937)
XLA Ops:
  7.9 0.8 broadcast_subtract_fusion
  8.7 1.6 fusion.56
  10.3 42.7 %while.14 = (s32[]{:T(128)}, f32[272,128]{1,0:T(8,128)S(1)}, f32[16,16384]{1,0:T(8,128)}, f32[16384]{0:T(1024)S(1)}, f32[16384]{0:T(1024)}, /*index=5*/s32[16384...) while((s32[]{:T(128)}, f32[272,128]{1,0:T(8,128)S(1)}, f32[16,16384]{1,0:T(8,128)}, ...), condition=%wide.region_1.2_spmd.clone, body=%wide.region_0.1_spmd.clone.sunk | while | flops 428839936 | bytes 4837545 | solution.py:91
  10.3 0.7 dynamic-slice_multiply_fusion.3
  11.0 0.8 broadcast_multiply_fusion.4
  12.1 0.8 convolution_add_fusion.2
  13.0 0.7 dynamic-slice_multiply_fusion.3
  13.7 0.8 broadcast_multiply_fusion.4
  14.8 0.8 convolution_add_fusion.2
  15.7 0.7 dynamic-slice_multiply_fusion.3
  16.3 0.8 broadcast_multiply_fusion.4
  17.5 0.8 convolution_add_fusion.2
  18.3 0.7 dynamic-slice_multiply_fusion.3
  19.0 0.8 broadcast_multiply_fusion.4
  20.1 0.8 convolution_add_fusion.2
  21.7 0.8 broadcast_multiply_fusion.4
  22.8 0.8 convolution_add_fusion.2
  23.7 0.7 dynamic-slice_multiply_fusion.3
  24.4 0.8 broadcast_multiply_fusion.4
  25.5 0.8 convolution_add_fusion.2
  27.0 0.8 broadcast_multiply_fusion.4
  28.1 0.8 convolution_add_fusion.2
  29.7 0.8 broadcast_multiply_fusion.4
  30.8 0.8 convolution_add_fusion.2
  32.4 0.8 broadcast_multiply_fusion.4
  33.5 0.8 convolution_add_fusion.2
  35.0 0.8 broadcast_multiply_fusion.4
  36.1 0.8 convolution_add_fusion.2
  37.7 0.8 broadcast_multiply_fusion.4
  38.8 0.8 convolution_add_fusion.2
  40.4 0.8 broadcast_multiply_fusion.4
  41.5 0.8 convolution_add_fusion.2
  43.0 0.8 broadcast_multiply_fusion.4
  44.1 0.8 convolution_add_fusion.2
  45.7 0.8 broadcast_multiply_fusion.4
  46.8 0.8 convolution_add_fusion.2
  48.4 0.8 broadcast_multiply_fusion.4
  49.5 0.8 convolution_add_fusion.2
  51.0 0.8 broadcast_multiply_fusion.4
  52.2 0.8 convolution_add_fusion.2
  54.9 90.6 %all-reduce.5.cloned.1.call-done = f32[272,128]{1,0:T(8,128)} async-done(((f32[272,128]{1,0:T(8,128)}), f32[272,128]{1,0:T(8,128)}) %all-reduce.5.cloned.1.call-update) | async-done | bytes 139280
  145.5 1.0 subtract_divide_fusion.110
  146.4 1.2 subtract_sqrt_fusion.8
  147.7 2.8 %subtract_divide_fusion.29 = (f32[8]{0:T(128)S(1)}, f32[8]{0:T(128)S(1)}, f32[8]{0:T(128)S(1)}, f32[8]{0:T(128)S(1)}, f32[8]{0:T(128)S(1)}, /*index=5*/f32[8]{0:...) fusion(f32[272,128]{1,0:T(8,128)} %all-reduce.5.cloned.1.call-d, ...), kind=kLoop, calls=%fused_computation.264 | loop fusion | flops 10472 | bytes 10624 | tf_op jit(solution)/shard_map/div | solution.py:38
  150.5 1.5 subtract_divide_fusion.15
  152.0 1.9 multiply_reduce_fusion
  154.6 1.4 fusion.9
  156.8 1.5 multiply_reduce_fusion.14
  158.2 1.4 multiply_reduce_fusion.15
  161.0 1.5 multiply_reduce_fusion.13
  163.2 1.5 multiply_reduce_fusion.12
  165.3 1.5 multiply_reduce_fusion.11
  167.5 1.5 multiply_reduce_fusion.10
  169.7 1.5 multiply_reduce_fusion.9
  171.8 1.5 multiply_reduce_fusion.8
  174.0 1.5 multiply_reduce_fusion.7
  176.2 1.5 multiply_reduce_fusion.6
  178.3 1.5 multiply_reduce_fusion.5
  180.5 1.5 multiply_reduce_fusion.4
  182.7 1.5 multiply_reduce_fusion.3
  184.8 1.5 multiply_reduce_fusion.2
  187.0 1.5 multiply_reduce_fusion.1
  190.5 5.5 %all-reduce.2 = (f32[]{:T(128)}, f32[]{:T(128)}) all-reduce(f32[]{:T(128)S(6)} %add.1130, f32[]{:T(128)} %get-tuple-element.154), channel_id=1, replica_groups=mesh['tm'=2,'src'=16] {'tm'}, use_global_device_ids=true, to_apply=%region_21.22 | all-reduce | flops 2 | bytes 16 | tf_op jit(solution)/shard_map/psum | solution.py:8
  196.0 31.2 %all-reduce.1 = (f32[]{:T(128)}, f32[]{:T(128)}) all-reduce(f32[]{:T(128)} %get-tuple-element.170, f32[]{:T(128)} %get-tuple-element.171), channel_id=1, replica_groups=mesh['tm'=2,'src'=16] {'src'}, use_global_device_ids=true, to_apply=%region_22.23 | all-reduce | flops 2 | bytes 16 | tf_op jit(solution)/shard_map/psum | solution.py:9
  (71 shorter events, 13.6 us)
Async XLA Ops:
  7.2 138.3 %all-reduce.5.cloned.1.call-start = ((), (), s32[]{:S(2)}) async-start(), calls=%async_computation | async-start | bytes 278528
  10.3 43.4 %copy-start.2 = (u32[32]{0:T(128)S(1)}, u32[32]{0:T(128)}, u32[]{:S(2)}) copy-start(u32[32]{0:T(128)} %constant.48) | copy-start | bytes 388
  10.3 135.2 %copy-start.1 = (f32[8]{0:T(128)S(1)}, f32[8]{0:T(128)}, u32[]{:S(2)}) copy-start(f32[8]{0:T(128)} %param.13) | copy-start | bytes 100
  53.0 0.7 copy-start
Sparse Core Ops, SparseCore 0:
  53.8 91.6 all-reduce.4
